TPU v7x, 32 devices: a whole 2x2x4 slice. The times are simulated.
32 devices in a mesh: grid: 8 (over y, x, core), rows: 4 (over z).
Axes of the slice: x: 2, y: 2, z: 4, core: 2. Of those that a mesh axis runs over, the one named last changes fastest.
Arguments:
- density: bfloat16 [32, 128, 4096], P(None, 'rows', 'grid'), as said below
- basis_values: bfloat16 [16, 16, 128, 512], P('grid', None, 'rows'), may hold values from -0.59765625 to 0.59765625
- grid_points: float32 [16, 3, 512], P('grid'), may hold values from -4 to 4
- grid_weights: float32 [16, 512], P('grid'), may hold values from 0.05 to 1
- screened_blocks: int32 [16, 16], P('grid'), may hold values from 0 to 31, as said below
Outputs:
- exchange: float32 [32, 128, 4096], P(None, 'rows', 'grid')
Inputs may be any that keep to these rules, and one draw needn't show every extreme that they name: density is symmetric: density[a, i, b * 128 + j] equals density[b, j, a * 128 + i]. `screened_blocks`: each row holds 16 distinct block numbers.
All inputs are finite; a program needn't handle non-finite values.
Results may differ from a plain program's by a relative error of at most 0.00055.
The roundings to bfloat16 on the way count: a program that leaves them out, or rounds other values in their place, can miss the bound.
Values may be sent and summed in bfloat16 or wider, within the bound.
A program may use at most 128 MiB of HBM per device.

v0:
```python
import jax
import jax.numpy as jnp
from jax import lax
from jax.sharding import PartitionSpec as P


def body(density, basis_values, grid_points, grid_weights, screened_blocks):
    nblocks = density.shape[0]
    rows_mine = density.shape[1]
    block_size = rows_mine * lax.axis_size("rows")
    nbasis = nblocks * block_size
    nsig = basis_values.shape[1]
    npoints = basis_values.shape[3]
    stripe = lax.all_gather(density, "grid", axis=2, tiled=True)
    totals = jnp.zeros((nblocks, rows_mine, nblocks, block_size), jnp.float32)
    for batch_index in range(basis_values.shape[0]):
        blocks = screened_blocks[batch_index]
        row_pick = jnp.take(stripe, blocks, axis=0).reshape(nsig * rows_mine, nblocks, block_size)
        chosen = jnp.take(row_pick, blocks, axis=1)
        local_values = basis_values[batch_index]
        x_mine = local_values.reshape(nsig * rows_mine, npoints)
        fsum = jnp.einsum(
            "mtk,tkp->mp",
            chosen,
            lax.all_gather(local_values, "rows", axis=1, tiled=True),
            preferred_element_type=jnp.float32,
        )
        fmat = fsum.astype(jnp.bfloat16)
        intersection_part = lax.dot_general(
            x_mine, fmat, (((0,), (0,)), ((), ())), preferred_element_type=jnp.float32
        )
        intersection = lax.psum(intersection_part, "rows")
        places = grid_points[batch_index]
        weights = grid_weights[batch_index]
        diffs = places[:, :, None] - places[:, None, :]
        kern = 1.0 / jnp.sqrt(jnp.sum(diffs * diffs, axis=0) + 0.5)
        mixed = (weights[:, None] * kern * intersection).astype(jnp.bfloat16)
        potential = (
            jnp.dot(x_mine, mixed, preferred_element_type=jnp.float32) * weights[None, :]
        ).astype(jnp.bfloat16)
        potential = potential.reshape(nsig, rows_mine, npoints)
        block_k = jnp.einsum(
            "mp,tkp->mtk",
            x_mine,
            lax.all_gather(potential, "rows", axis=1, tiled=True),
            preferred_element_type=jnp.float32,
        )
        block_k = block_k.reshape(nsig, rows_mine, nsig, block_size)
        totals = totals.at[blocks[:, None], :, blocks[None, :], :].add(
            block_k.transpose(0, 2, 1, 3)
        )
    return lax.psum_scatter(
        totals.reshape(nblocks, rows_mine, nbasis), "grid", scatter_dimension=2, tiled=True
    )


def solution(mesh):
    placed = (
        P(None, "rows", "grid"),
        P("grid", None, "rows", None),
        P("grid", None, None),
        P("grid", None),
        P("grid", None),
    )
    return jax.shard_map(
        body, mesh=mesh, in_specs=placed, out_specs=P(None, "rows", "grid"), check_vma=False
    )
```

profile of v0, /device:TPU:0, one launch (start us, length us, event | category | flops | bytes accessed | tf_op | source)
XLA Modules:
  0.0 572.5 jit_solution(16403228100501752769)
XLA Ops:
  7.3 2.3 fusion.56
  10.5 57.3 %all-gather.8.cloned.1.call-done = bf16[32,32,4096]{2,1,0:T(8,128)(2,1)} async-done(((bf16[32,32,512]{2,1,0:T(8,128)(2,1)}), bf16[32,32,4096]{2,1,0:T(8,128)(2,1)}) %all-gather.8.cloned.1.call-update) | async-done | bytes 8388624 | tf_op jit(solution)/shard_map/all_gather | solution.py:14
  67.8 6.2 %gather_fusion.2 = bf16[16,32,4096]{2,1,0:T(8,128)(2,1)} fusion(bf16[32,32,4096]{2,1,0:T(8,128)(2,1)} %all-gather.8.cloned.1.call-done, s32[1024]{0:T(1024)S(1)} %pad_clamp_fusion), kind=kCustom, calls=%fused_computation.2.clone | custom fusion | bytes 8388672 | tf_op jit(solution)/shard_map/jit(_take)/gather | solution.py:18
  74.0 2.7 broadcast_select_fusion
  76.7 1.3 copy.31
  78.0 3.6 copy.23
  81.6 3.1 gather_fusion.3
  84.8 6.2 %gather_fusion = bf16[16,32,4096]{2,1,0:T(8,128)(2,1)} fusion(bf16[32,32,4096]{2,1,0:T(8,128)(2,1)} %all-gather.8.cloned.1.call-done, s32[1024]{0:T(1024)S(1)} %pad_clamp_fusion.1), kind=kCustom, calls=%fused_computation.clone | custom fusion | bytes 8388672 | tf_op jit(solution)/shard_map/jit(_take)/gather | solution.py:18
  91.0 2.7 broadcast_select_fusion.1
  93.6 1.3 copy.30
  94.9 3.6 copy.19
  98.5 4.4 gather_fusion.1
  102.9 12.2 %all-gather.16.cloned.1.call-done = bf16[1,16,128,512]{3,2,1,0:T(8,128)(2,1)} async-done(((bf16[1,16,32,512]{3,2,1,0:T(8,128)(2,1)}), bf16[1,16,128,512]{3,2,1,0:T(8,128)(2,1)}) %all-gather.16.cloned.1.call-update) | async-done | bytes 2097168 | tf_op jit(solution)/shard_map/all_gather | solution.py:25
  115.1 4.3 convolution_bitcast_fusion.2
  119.4 41.8 %all-gather.14.cloned.1.call-done = bf16[1,16,128,512]{3,2,1,0:T(8,128)(2,1)} async-done(((bf16[1,16,32,512]{3,2,1,0:T(8,128)(2,1)}), bf16[1,16,128,512]{3,2,1,0:T(8,128)(2,1)}) %all-gather.14.cloned.1.call-update) | async-done | bytes 2097168 | tf_op jit(solution)/shard_map/all_gather | solution.py:25
  161.2 4.9 convolution_bitcast_fusion.3
  166.9 84.3 %all-reduce.3.cloned.1.call-done = (f32[512,512]{0,1:T(8,128)}, f32[512,512]{0,1:T(8,128)}) async-done(((f32[512,512]{0,1:T(8,128)}, f32[512,512]{0,1:T(8,128)}), (f32[512,512]{0,1:T(8,128)}, f32[512,512]{0,1:T(8,128)})) %all-reduce.3.cloned.1.call-update) | async-done | bytes 2097168 | tf_op jit(solution)/shard_map/psum | solution.py:32
  251.2 2.5 fusion.20
  254.5 2.5 fusion.21
  257.6 41.0 %all-gather.10.cloned.1.call-done = bf16[16,128,512]{2,1,0:T(8,128)(2,1)} async-done(((bf16[16,32,512]{2,1,0:T(8,128)(2,1)}), bf16[16,128,512]{2,1,0:T(8,128)(2,1)}) %all-gather.10.cloned.1.call-update) | async-done | bytes 2097168 | tf_op jit(solution)/shard_map/all_gather | solution.py:45
  298.6 4.8 convolution_bitcast_fusion.1
  303.4 5.5 copy.20
  309.0 5.5 copy.21
  314.4 30.1 %all-gather.12.cloned.1.call-done = bf16[16,128,512]{2,1,0:T(8,128)(2,1)} async-done(((bf16[16,32,512]{2,1,0:T(8,128)(2,1)}), bf16[16,128,512]{2,1,0:T(8,128)(2,1)}) %all-gather.12.cloned.1.call-update) | async-done | bytes 2097168 | tf_op jit(solution)/shard_map/all_gather | solution.py:45
  344.5 4.8 convolution_bitcast_fusion
  349.3 5.5 copy.24
  354.8 5.5 copy.25
  360.3 7.9 %broadcast_in_dim.45 = f32[32,32,32,128]{3,1,2,0:T(8,128)} broadcast(f32[]{:T(128)} %constant.20.clone.1), dimensions={} | broadcast | bytes 16777220 | tf_op jit(solution)/shard_map/broadcast_in_dim | solution.py:15
  368.2 35.3 %scatter_fusion = f32[32,32,32,128]{3,1,2,0:T(8,128)} fusion(f32[32,32,32,128]{3,1,2,0:T(8,128)} %broadcast_in_dim.45, s32[256]{0:T(256)S(1)} %reshape.132, f32[256,32,128]{2,1,0:T(8,128)} %bitcast.123), kind=kCustom, calls=%fused_computation.4 | custom fusion | flops 1048576 | bytes 12584960 | tf_op jit(solution)/shard_map/scatter-add | solution.py:49
  403.5 35.3 %scatter_fusion.1 = f32[32,32,32,128]{3,1,2,0:T(8,128)} fusion(f32[32,32,32,128]{3,1,2,0:T(8,128)} %scatter_fusion, s32[256]{0:T(256)S(1)} %reshape.138, f32[256,32,128]{2,1,0:T(8,128)} %bitcast.124), kind=kCustom, calls=%fused_computation.5 | custom fusion | flops 1048576 | bytes 12584960 | tf_op jit(solution)/shard_map/scatter-add | solution.py:49
  438.9 11.7 %copy_bitcast_fusion = f32[32,32,4096]{2,1,0:T(8,128)} fusion(f32[32,32,32,128]{3,1,2,0:T(8,128)} %scatter_fusion.1), kind=kLoop, calls=%fused_computation.6 | loop fusion | bytes 33554432 | tf_op jit(solution)/shard_map/reshape | solution.py:53
  450.6 115.0 %reduce-scatter.2.cloned.1.call-done = f32[32,32,512]{2,1,0:T(8,128)} async-done(((f32[32,32,4096]{2,1,0:T(8,128)}), f32[32,32,512]{2,1,0:T(8,128)}) %reduce-scatter.2.cloned.1.call-update) | async-done | bytes 2097168 | tf_op jit(solution)/shard_map/reduce_scatter | solution.py:52
  (42 shorter events, 3.6 us)
Async XLA Ops:
  6.5 3.9 copy-start.4
  6.5 61.3 %all-gather.8.cloned.1.call-start = ((), (), s32[]{:S(2)}) async-start(), calls=%async_computation.1 | async-start | bytes 9437184 | tf_op jit(solution)/shard_map/all_gather | solution.py:14
  7.3 107.8 %all-gather.16.cloned.1.call-start = ((), (), s32[]{:S(2)}) async-start(), calls=%async_computation.6 | async-start | bytes 2621440 | tf_op jit(solution)/shard_map/all_gather | solution.py:25
  9.6 151.5 %all-gather.14.cloned.1.call-start = ((), (), s32[]{:S(2)}) async-start(), calls=%async_computation.5 | async-start | bytes 2621440 | tf_op jit(solution)/shard_map/all_gather | solution.py:25
  10.4 240.8 %all-reduce.3.cloned.1.call-start = ((), (), s32[]{:S(2)}) async-start(), calls=%async_computation.7 | async-start | bytes 4194304 | tf_op jit(solution)/shard_map/psum | solution.py:32
  98.5 16.6 %copy-start = (bf16[1,16,32,512]{3,2,1,0:T(8,128)(2,1)S(1)}, bf16[1,16,32,512]{3,2,1,0:T(8,128)(2,1)}, u32[]{:S(2)}) copy-start(bf16[1,16,32,512]{3,2,1,0:T(8,128)(2,1)} %get-tuple-element.13) | copy-start | bytes 1572868
  115.1 46.1 %copy-start.1 = (bf16[1,16,32,512]{3,2,1,0:T(8,128)(2,1)S(1)}, bf16[1,16,32,512]{3,2,1,0:T(8,128)(2,1)}, u32[]{:S(2)}) copy-start(bf16[1,16,32,512]{3,2,1,0:T(8,128)(2,1)} %get-tuple-element.14) | copy-start | bytes 1572868
  161.2 5.0 copy-start.2
  166.0 0.8 copy-start.3
  166.1 132.5 %all-gather.10.cloned.1.call-start = ((), (), s32[]{:S(2)}) async-start(), calls=%async_computation.2 | async-start | bytes 2621440 | tf_op jit(solution)/shard_map/all_gather | solution.py:45
  253.7 90.8 %all-gather.12.cloned.1.call-start = ((), (), s32[]{:S(2)}) async-start(), calls=%async_computation.3 | async-start | bytes 2621440 | tf_op jit(solution)/shard_map/all_gather | solution.py:45
  257.0 308.6 %reduce-scatter.2.cloned.1.call-start = ((), (), s32[]{:S(2)}) async-start(), calls=%async_computation.4 | async-start | bytes 18874368 | tf_op jit(solution)/shard_map/reduce_scatter | solution.py:52
Sparse Core Ops, SparseCore 0:
  9.2 58.5 all-gather.7
  69.4 45.6 all-gather.15
  116.7 44.4 all-gather.13
  166.2 84.9 all-reduce.2
  253.9 44.6 all-gather.9
  300.0 44.4 all-gather.11
  450.7 114.8 reduce-scatter.1
where the time goes:
time: 574 us; the launch traced here: 572 us
  waiting for transfers between devices  383 us (67%)
  other arithmetic  76.9 us (13%)
  local copies, waits for them, and re-layouts  74.4 us (13%)
  matrix products  23.9 us (4%)
  between operations  13.7 us (2%)
    reduce_scatter x1, waiting for transfers between devices, body(): lax.psum_scatter(totals.reshape(nblocks, rows_mine, nbasis), 'grid', scat...  115 us
    psum x1, waiting for transfers between devices, body(): intersection = lax.psum(intersection_part, 'rows')  84.3 us
    all_gather x2, waiting for transfers between devices, body(): lax.all_gather(potential, 'rows', axis=1, tiled=True)  71.1 us
    scatter-add x2, other arithmetic, body(): totals.at[blocks[:, None], :, blocks[None, :], :]  70.6 us
    all_gather x1, waiting for transfers between devices, body(): stripe = lax.all_gather(density, 'grid', axis=2, tiled=True)  57.3 us
    all_gather x2, waiting for transfers between devices, body(): lax.all_gather(local_values, 'rows', axis=1, tiled=True)  53.9 us
    gather x2, local copies, waits for them, and re-layouts, body(): jnp.take(stripe, blocks, axis=0)  12.4 us
    reshape x1, local copies, waits for them, and re-layouts, body(): totals.reshape(nblocks, rows_mine, nbasis)  11.7 us
  transfers between devices with their start and end apart: 7, of which 7 were waited for; matrix products, arithmetic and copies ran while one was open for 11% of the time, Pallas kernels for 0%

commit v1 on v0

--- a/solution.py
+++ b/solution.py
@@ -19,12 +19,27 @@
         chosen = jnp.take(row_pick, blocks, axis=1)
         local_values = basis_values[batch_index]
         x_mine = local_values.reshape(nsig * rows_mine, npoints)
-        fsum = jnp.einsum(
+        size, index = (lax.axis_size("rows"), lax.axis_index("rows"))
+        backward = [(i, (i - 1) % size) for i in range(size)]
+        rows = local_values.shape[1]
+        held = local_values
+        subtotal = jnp.einsum(
             "mtk,tkp->mp",
-            chosen,
-            lax.all_gather(local_values, "rows", axis=1, tiled=True),
+            lax.dynamic_slice_in_dim(chosen, index * rows, held.shape[1], axis=2),
+            held,
             preferred_element_type=jnp.float32,
         )
+        for step in range(1, size):
+            held = lax.ppermute(held, "rows", backward)
+            subtotal = subtotal + jnp.einsum(
+                "mtk,tkp->mp",
+                lax.dynamic_slice_in_dim(
+                    chosen, (index + step) % size * rows, held.shape[1], axis=2
+                ),
+                held,
+                preferred_element_type=jnp.float32,
+            )
+        fsum = subtotal
         fmat = fsum.astype(jnp.bfloat16)
         intersection_part = lax.dot_general(
             x_mine, fmat, (((0,), (0,)), ((), ())), preferred_element_type=jnp.float32

time: 574 us -> 536 us (0.934)
  waiting for transfers between devices: 383 us -> 308 us
  starting transfers between devices: 0.43 us -> 23.3 us
    all_gather x2 -> x0, waiting for transfers between devices: 53.9 us -> none  [body(): lax.all_gather(local_values, 'rows', axis=1, tiled=True)]
    all_gather x1, waiting for transfers between devices: 57.3 us -> 3.5 us  [body(): stripe = lax.all_gather(density, 'grid', axis=2, tiled=True)]
    ppermute x0 -> x6, waiting for transfers between devices: none -> 32.6 us  [body(): held = lax.ppermute(held, 'rows', backward)]
    ppermute x0 -> x6, starting transfers between devices: none -> 22.9 us  [body(): held = lax.ppermute(held, 'rows', backward)]
    dot_general x0 -> x6, matrix products: none -> 6.85 us  [the longest x4 5.91 us: body(): jnp.einsum('mtk,tkp->mp', lax.dynamic_slice_in_dim(chosen, (index + step)...]
  transfers between devices with their start and end apart: 7 -> 11, of which waited for: 7 -> 9; matrix products, arithmetic and copies ran while one was open for 11% -> 14% of each run, Pallas kernels for 0% -> 0%
where the time goes in v1:
time: 536 us; the launch traced here: 535 us
  waiting for transfers between devices  308 us (57%)
  other arithmetic  82.1 us (15%)
  local copies, waits for them, and re-layouts  79.3 us (15%)
  matrix products  28.2 us (5%)
  starting transfers between devices  23.3 us (4%)
  between operations  13.4 us (2%)
    reduce_scatter x1, waiting for transfers between devices, body(): lax.psum_scatter(totals.reshape(nblocks, rows_mine, nbasis), 'grid', scat...  115 us
    psum x1, waiting for transfers between devices, body(): intersection = lax.psum(intersection_part, 'rows')  85.3 us
    all_gather x2, waiting for transfers between devices, body(): lax.all_gather(potential, 'rows', axis=1, tiled=True)  71.3 us
    scatter-add x2, other arithmetic, body(): totals.at[blocks[:, None], :, blocks[None, :], :]  70.7 us
    ppermute x6, waiting for transfers between devices, body(): held = lax.ppermute(held, 'rows', backward)  32.6 us
    ppermute x6, starting transfers between devices, body(): held = lax.ppermute(held, 'rows', backward)  22.9 us
    gather x2, local copies, waits for them, and re-layouts, body(): jnp.take(stripe, blocks, axis=0)  12.3 us
    reshape x1, local copies, waits for them, and re-layouts, body(): totals.reshape(nblocks, rows_mine, nbasis)  11.7 us
  transfers between devices with their start and end apart: 11, of which 9 were waited for; matrix products, arithmetic and copies ran while one was open for 14% of the time, Pallas kernels for 0%

profile of v1, /device:TPU:0, one launch (start us, length us, event | category | flops | bytes accessed | tf_op | source)
XLA Modules:
  0.0 534.5 jit_solution(6353247759422143915)
XLA Ops:
  8.8 5.1 collective-permute-start.3
  14.4 11.9 %collective-permute-done.3 = bf16[16,32,512]{2,1,0:T(8,128)(2,1)S(1)} collective-permute-done((bf16[16,32,512]{2,1,0:T(8,128)(2,1)S(1)}, bf16[16,32,512]{2,1,0:T(8,128)(2,1)S(1)}, u32[]{:S(2)}, u32[]{:S(2)}) %collective-permute-start.3) | collective-permute-done | bytes 524320 | tf_op jit(solution)/shard_map/ppermute | solution.py:33
  26.2 4.3 collective-permute-start.4
  30.5 7.0 %collective-permute-done = bf16[16,32,512]{2,1,0:T(8,128)(2,1)S(1)} collective-permute-done((bf16[16,32,512]{2,1,0:T(8,128)(2,1)S(1)}, bf16[16,32,512]{2,1,0:T(8,128)(2,1)S(1)}, u32[]{:S(2)}, u32[]{:S(2)}) %collective-permute-start) | collective-permute-done | bytes 524320 | tf_op jit(solution)/shard_map/ppermute | solution.py:33
  37.5 4.3 collective-permute-start.1
  41.8 6.9 %collective-permute-done.4 = bf16[16,32,512]{2,1,0:T(8,128)(2,1)} collective-permute-done((bf16[16,32,512]{2,1,0:T(8,128)(2,1)S(1)}, bf16[16,32,512]{2,1,0:T(8,128)(2,1)}, u32[]{:S(2)}, u32[]{:S(2)}) %collective-permute-start.4) | collective-permute-done | bytes 524320 | tf_op jit(solution)/shard_map/ppermute | solution.py:33
  48.7 4.4 collective-permute-start.5
  53.1 6.9 %collective-permute-done.1 = bf16[16,32,512]{2,1,0:T(8,128)(2,1)} collective-permute-done((bf16[16,32,512]{2,1,0:T(8,128)(2,1)S(1)}, bf16[16,32,512]{2,1,0:T(8,128)(2,1)}, u32[]{:S(2)}, u32[]{:S(2)}) %collective-permute-start.1) | collective-permute-done | bytes 524320 | tf_op jit(solution)/shard_map/ppermute | solution.py:33
  60.0 4.4 collective-permute-start.2
  64.3 3.5 all-gather.4.cloned.1.call-done
  67.8 6.2 %gather_fusion.2 = bf16[16,32,4096]{2,1,0:T(8,128)(2,1)} fusion(bf16[32,32,4096]{2,1,0:T(8,128)(2,1)} %all-gather.4.cloned.1.call-done, s32[1024]{0:T(1024)S(1)} %get-tuple-element.31), kind=kCustom, calls=%fused_computation.2.clone | custom fusion | bytes 8388672 | tf_op jit(solution)/shard_map/jit(_take)/gather | solution.py:18
  77.9 3.6 copy.26
  81.5 3.1 gather_fusion.3
  87.3 3.2 select_bitcast_fusion
  90.5 6.2 %gather_fusion = bf16[16,32,4096]{2,1,0:T(8,128)(2,1)} fusion(bf16[32,32,4096]{2,1,0:T(8,128)(2,1)} %all-gather.4.cloned.1.call-done, s32[1024]{0:T(1024)S(1)} %get-tuple-element.32), kind=kCustom, calls=%fused_computation.clone | custom fusion | bytes 8388672 | tf_op jit(solution)/shard_map/jit(_take)/gather | solution.py:18
  100.6 3.6 copy.21
  120.6 3.2 convolution_bitcast_fusion.2
  123.9 3.4 convolution_bitcast_fusion.7
  128.3 85.3 %all-reduce.3.cloned.1.call-done = (f32[512,512]{0,1:T(8,128)}, f32[512,512]{0,1:T(8,128)}) async-done(((f32[512,512]{0,1:T(8,128)}, f32[512,512]{0,1:T(8,128)}), (f32[512,512]{0,1:T(8,128)}, f32[512,512]{0,1:T(8,128)})) %all-reduce.3.cloned.1.call-update) | async-done | bytes 2097168 | tf_op jit(solution)/shard_map/psum | solution.py:47
  219.9 41.1 %all-gather.6.cloned.1.call-done = bf16[16,128,512]{2,1,0:T(8,128)(2,1)} async-done(((bf16[16,32,512]{2,1,0:T(8,128)(2,1)}), bf16[16,128,512]{2,1,0:T(8,128)(2,1)}) %all-gather.6.cloned.1.call-update) | async-done | bytes 2097168 | tf_op jit(solution)/shard_map/all_gather | solution.py:60
  261.0 4.8 convolution_bitcast_fusion.1
  265.8 5.6 %copy.23 = f32[512,16,128]{2,1,0:T(8,128)} copy(f32[512,16,128]{0,2,1:T(8,128)} %convolution_bitcast_fusion.1) | data formatting | bytes 8388608 | tf_op jit(solution)/shard_map/mp,tkp->mtk/dot_general | solution.py:57
  271.4 5.4 %copy.24 = f32[16,16,32,128]{3,2,1,0:T(8,128)} copy(f32[16,16,32,128]{3,1,2,0:T(8,128)} %bitcast.135) | data formatting | bytes 8388608 | tf_op jit(solution)/shard_map/transpose | solution.py:65
  276.8 30.1 %all-gather.8.cloned.1.call-done = bf16[16,128,512]{2,1,0:T(8,128)(2,1)} async-done(((bf16[16,32,512]{2,1,0:T(8,128)(2,1)}), bf16[16,128,512]{2,1,0:T(8,128)(2,1)}) %all-gather.8.cloned.1.call-update) | async-done | bytes 2097168 | tf_op jit(solution)/shard_map/all_gather | solution.py:60
  306.9 4.8 convolution_bitcast_fusion
  311.7 5.5 %copy.28 = f32[512,16,128]{2,1,0:T(8,128)} copy(f32[512,16,128]{0,2,1:T(8,128)} %convolution_bitcast_fusion) | data formatting | bytes 8388608 | tf_op jit(solution)/shard_map/mp,tkp->mtk/dot_general | solution.py:57
  317.3 5.5 %copy.29 = f32[16,16,32,128]{3,2,1,0:T(8,128)} copy(f32[16,16,32,128]{3,1,2,0:T(8,128)} %bitcast.136) | data formatting | bytes 8388608 | tf_op jit(solution)/shard_map/transpose | solution.py:65
  322.8 7.9 %broadcast_in_dim.45 = f32[32,32,32,128]{3,1,2,0:T(8,128)} broadcast(f32[]{:T(128)} %constant.42.clone.1), dimensions={} | broadcast | bytes 16777220 | tf_op jit(solution)/shard_map/broadcast_in_dim | solution.py:15
  330.6 35.3 %scatter_fusion = f32[32,32,32,128]{3,1,2,0:T(8,128)} fusion(f32[32,32,32,128]{3,1,2,0:T(8,128)} %broadcast_in_dim.45, s32[256]{0:T(256)S(1)} %reshape.132, f32[256,32,128]{2,1,0:T(8,128)} %bitcast.129), kind=kCustom, calls=%fused_computation.4 | custom fusion | flops 1048576 | bytes 12584960 | tf_op jit(solution)/shard_map/scatter-add | solution.py:64
  365.9 35.4 %scatter_fusion.1 = f32[32,32,32,128]{3,1,2,0:T(8,128)} fusion(f32[32,32,32,128]{3,1,2,0:T(8,128)} %scatter_fusion, s32[256]{0:T(256)S(1)} %reshape.138, f32[256,32,128]{2,1,0:T(8,128)} %bitcast.130), kind=kCustom, calls=%fused_computation.5 | custom fusion | flops 1048576 | bytes 12584960 | tf_op jit(solution)/shard_map/scatter-add | solution.py:64
  401.4 11.7 %copy_bitcast_fusion = f32[32,32,4096]{2,1,0:T(8,128)} fusion(f32[32,32,32,128]{3,1,2,0:T(8,128)} %scatter_fusion.1), kind=kLoop, calls=%fused_computation.6 | loop fusion | bytes 33554432 | tf_op jit(solution)/shard_map/reshape | solution.py:68
  413.1 114.9 %reduce-scatter.2.cloned.1.call-done = f32[32,32,512]{2,1,0:T(8,128)} async-done(((f32[32,32,4096]{2,1,0:T(8,128)}), f32[32,32,512]{2,1,0:T(8,128)}) %reduce-scatter.2.cloned.1.call-update) | async-done | bytes 2097168 | tf_op jit(solution)/shard_map/reduce_scatter | solution.py:67
  (67 shorter events, 36.8 us)
Async XLA Ops:
  6.5 35.2 %copy-start.5 = (s32[2,16]{1,0:T(2,128)S(1)}, s32[2,16]{1,0:T(2,128)}, u32[]{:S(2)}) copy-start(s32[2,16]{1,0:T(2,128)} %param.13) | copy-start | bytes 388
  6.5 61.3 %all-gather.4.cloned.1.call-start = ((), (), s32[]{:S(2)}) async-start(), calls=%async_computation.1 | async-start | bytes 9437184 | tf_op jit(solution)/shard_map/all_gather | solution.py:14
  7.3 206.4 %all-reduce.3.cloned.1.call-start = ((), (), s32[]{:S(2)}) async-start(), calls=%async_computation.5 | async-start | bytes 4194304 | tf_op jit(solution)/shard_map/psum | solution.py:47
  8.8 17.4 %collective-permute-start.3 = (bf16[16,32,512]{2,1,0:T(8,128)(2,1)S(1)}, bf16[16,32,512]{2,1,0:T(8,128)(2,1)S(1)}, u32[]{:S(2)}, u32[]{:S(2)}) collective-permute-start(bf16[16,32,512]{2,1,0:T(8,128)(2,1)S(1)} %get-tuple-element.13), channel_id=1, source_target_pairs={{0,3},{1,0},{2,1},{3,2},{4,7},{5,4},{6,5},{7,6},{8,11},{9,8},{10,9... | collective-permute-start | bytes 1572872 | tf_op jit(solution)/shard_map/ppermute | solution.py:33
  13.9 23.5 %collective-permute-start = (bf16[16,32,512]{2,1,0:T(8,128)(2,1)S(1)}, bf16[16,32,512]{2,1,0:T(8,128)(2,1)S(1)}, u32[]{:S(2)}, u32[]{:S(2)}) collective-permute-start(bf16[16,32,512]{2,1,0:T(8,128)(2,1)S(1)} %get-tuple-element.14), channel_id=1, source_target_pairs={{0,3},{1,0},{2,1},{3,2},{4,7},{5,4},{6,5},{7,6},{8,11},{9,8},{10,9... | collective-permute-start | bytes 1572872 | tf_op jit(solution)/shard_map/ppermute | solution.py:33
  26.2 47.8 %copy-start.6 = (bf16[16,32,512]{2,1,0:T(8,128)(2,1)}, bf16[16,32,512]{2,1,0:T(8,128)(2,1)S(1)}, u32[]{:S(2)}) copy-start(bf16[16,32,512]{2,1,0:T(8,128)(2,1)S(1)} %collective-permute-done.3) | copy-start | bytes 1572868
  26.2 22.5 %collective-permute-start.4 = (bf16[16,32,512]{2,1,0:T(8,128)(2,1)S(1)}, bf16[16,32,512]{2,1,0:T(8,128)(2,1)}, u32[]{:S(2)}, u32[]{:S(2)}) collective-permute-start(bf16[16,32,512]{2,1,0:T(8,128)(2,1)S(1)} %collective-permute-done.3), channel_id=1, source_target_pairs={{0,3},{1,0},{2,1},{3,2},{4,7},{5,4},{6,5},{7,6},{8,11},{9,8},{10,9... | collective-permute-start | bytes 1572872 | tf_op jit(solution)/shard_map/ppermute | solution.py:33
  37.5 36.5 %copy-start.8 = (bf16[16,32,512]{2,1,0:T(8,128)(2,1)}, bf16[16,32,512]{2,1,0:T(8,128)(2,1)S(1)}, u32[]{:S(2)}) copy-start(bf16[16,32,512]{2,1,0:T(8,128)(2,1)S(1)} %collective-permute-done) | copy-start | bytes 1572868
  37.5 22.5 %collective-permute-start.1 = (bf16[16,32,512]{2,1,0:T(8,128)(2,1)S(1)}, bf16[16,32,512]{2,1,0:T(8,128)(2,1)}, u32[]{:S(2)}, u32[]{:S(2)}) collective-permute-start(bf16[16,32,512]{2,1,0:T(8,128)(2,1)S(1)} %collective-permute-done), channel_id=1, source_target_pairs={{0,3},{1,0},{2,1},{3,2},{4,7},{5,4},{6,5},{7,6},{8,11},{9,8},{10,9... | collective-permute-start | bytes 1572872 | tf_op jit(solution)/shard_map/ppermute | solution.py:33
  48.7 71.9 %collective-permute-start.5 = (bf16[16,32,512]{2,1,0:T(8,128)(2,1)}, bf16[16,32,512]{2,1,0:T(8,128)(2,1)}, u32[]{:S(2)}, u32[]{:S(2)}) collective-permute-start(bf16[16,32,512]{2,1,0:T(8,128)(2,1)} %collective-permute-done.4), channel_id=1, source_target_pairs={{0,3},{1,0},{2,1},{3,2},{4,7},{5,4},{6,5},{7,6},{8,11},{9,8},{10,9... | collective-permute-start | bytes 1572872 | tf_op jit(solution)/shard_map/ppermute | solution.py:33
  60.0 63.9 %collective-permute-start.2 = (bf16[16,32,512]{2,1,0:T(8,128)(2,1)}, bf16[16,32,512]{2,1,0:T(8,128)(2,1)}, u32[]{:S(2)}, u32[]{:S(2)}) collective-permute-start(bf16[16,32,512]{2,1,0:T(8,128)(2,1)} %collective-permute-done.1), channel_id=1, source_target_pairs={{0,3},{1,0},{2,1},{3,2},{4,7},{5,4},{6,5},{7,6},{8,11},{9,8},{10,9... | collective-permute-start | bytes 1572872 | tf_op jit(solution)/shard_map/ppermute | solution.py:33
  109.9 2.2 copy-start
  109.9 2.5 copy-start.2
  112.3 5.8 %copy-start.1 = (bf16[512,16,128]{0,2,1:T(8,128)(2,1)}, bf16[512,16,128]{0,2,1:T(8,128)(2,1)S(1)}, u32[]{:S(2)}) copy-start(bf16[512,16,128]{0,2,1:T(8,128)(2,1)S(1)} %select_bitcast_fusion.1) | copy-start | bytes 6291460
  112.8 1.3 copy-start.7
  114.1 1.0 copy-start.9
  123.9 3.7 copy-start.3
  127.3 1.0 copy-start.4
  127.3 133.7 %all-gather.6.cloned.1.call-start = ((), (), s32[]{:S(2)}) async-start(), calls=%async_computation.2 | async-start | bytes 2621440 | tf_op jit(solution)/shard_map/all_gather | solution.py:60
  216.2 90.8 %all-gather.8.cloned.1.call-start = ((), (), s32[]{:S(2)}) async-start(), calls=%async_computation.3 | async-start | bytes 2621440 | tf_op jit(solution)/shard_map/all_gather | solution.py:60
  219.5 308.5 %reduce-scatter.2.cloned.1.call-start = ((), (), s32[]{:S(2)}) async-start(), calls=%async_computation.4 | async-start | bytes 18874368 | tf_op jit(solution)/shard_map/reduce_scatter | solution.py:67
Sparse Core Ops, SparseCore 0:
  9.2 58.5 all-gather.3
  127.4 86.1 all-reduce.2
  216.3 44.6 all-gather.5
  262.4 44.4 all-gather.7
  413.2 114.7 reduce-scatter.1
